TPU v7x, 32 devices: a whole 2x2x4 slice. The times are simulated.
32 devices in a mesh: seq: 8 (over z, x), fsdp: 4 (over y, core).
Axes of the slice: x: 2, y: 2, z: 4, core: 2. Of those that a mesh axis runs over, the one named last changes fastest.
Arguments:
- tokens: bfloat16 [4, 1024, 1536], P('fsdp', 'seq'), may hold values from -6 to 6
- in_weight: bfloat16 [1536, 6400], P('fsdp'), may hold values from -0.15625 to 0.15625
- step_weight: bfloat16 [1536, 48], P('fsdp'), may hold values from -0.15625 to 0.15625
- conv_kernel: bfloat16 [4, 3328], P(None, 'fsdp'), may hold values from -3 to 3
- conv_bias: bfloat16 [3328], P('fsdp'), may hold values from -3 to 3
- step_bias: bfloat16 [48], P('fsdp'), may hold values from -6 to -3
- log_decay: bfloat16 [48], P('fsdp'), may hold values from -7 to 1
- skip_gain: bfloat16 [48], P('fsdp'), may hold values from 0.5 to 1.5
- gate_gain: bfloat16 [3072], P('fsdp'), may hold values from 0.5 to 1.5
- norm_gain: bfloat16 [1536], P('fsdp'), may hold values from 0.5 to 1.5
- out_weight: bfloat16 [3072, 1536], P('fsdp'), may hold values from -0.109375 to 0.109375
- cotangent: bfloat16 [4, 1024, 1536], P('fsdp', 'seq'), may hold values from -6 to 6
Outputs:
- block_out: bfloat16 [4, 1024, 1536], P('fsdp', 'seq')
- input_grad: float32 [4, 1024, 1536], P('fsdp', 'seq')
- in_weight_grad: float32 [1536, 6400], P('fsdp')
- step_weight_grad: float32 [1536, 48], P('fsdp')
- conv_kernel_grad: float32 [4, 3328], P(None, 'fsdp')
- conv_bias_grad: float32 [3328], P('fsdp')
- step_bias_grad: float32 [48], P('fsdp')
- log_decay_grad: float32 [48], P('fsdp')
- skip_gain_grad: float32 [48], P('fsdp')
- gate_gain_grad: float32 [3072], P('fsdp')
- norm_gain_grad: float32 [1536], P('fsdp')
- out_weight_grad: float32 [3072, 1536], P('fsdp')
All inputs are finite; a program needn't handle non-finite values.
Results may differ from a plain program's by a relative error of at most 0.012.
The roundings to bfloat16 on the way count: a program that leaves them out, or rounds other values in their place, can miss the bound.
Values may be sent and summed in bfloat16 or wider, within the bound.
A program may use at most 320 MiB of HBM per device.

v0:
```python
import jax
import jax.numpy as jnp
from jax import lax
from jax.sharding import PartitionSpec as P

N = 128
BLOCK = 256
epsilon = 1e-05
highest = lax.Precision.HIGHEST


def block_step(carried, pieces, decay_rate):
    x_blk, step_blk, b_blk, c_blk = pieces
    cumulative = jnp.cumsum(step_blk * decay_rate[None, :], axis=0).T
    positions = jnp.arange(step_blk.shape[0])
    triangle = positions[:, None] >= positions[None, :]
    log_gap = jnp.where(triangle[None], cumulative[:, :, None] - cumulative[:, None, :], -1e30)
    scores = jnp.dot(c_blk, b_blk.T, precision=highest)
    mixing = jnp.exp(log_gap) * scores[None] * step_blk.T[:, None, :]
    y_inside = jnp.einsum("hij,jhp->ihp", mixing, x_blk, precision=highest)
    y_carried = jnp.exp(cumulative).T[:, :, None] * jnp.einsum(
        "in,hpn->ihp", c_blk, carried, precision=highest
    )
    weighting = jnp.exp(cumulative[:, -1:] - cumulative) * step_blk.T
    renewed = jnp.exp(cumulative[:, -1])[:, None, None] * carried + jnp.einsum(
        "hj,jhp,jn->hpn", weighting, x_blk, b_blk, precision=highest
    )
    return (renewed, y_inside + y_carried)


def ssd_scan(x_heads, step_size, decay_rate, b_conv, c_conv, carried):
    length = step_size.shape[0]
    extent = min(BLOCK, length)
    number = length // extent
    pieces = (
        x_heads.reshape((number, extent) + x_heads.shape[1:]),
        step_size.reshape((number, extent) + step_size.shape[1:]),
        b_conv.reshape(number, extent, -1),
        c_conv.reshape(number, extent, -1),
    )

    def advance(ssm_state, block_in):
        return block_step(ssm_state, block_in, decay_rate)

    finals, outputs = lax.scan(jax.checkpoint(advance), carried, pieces)
    return outputs.reshape(x_heads.shape)


def prepare(extended, raw_steps, conv_kernel, conv_offset, step_bias, log_rates):
    kernel_width = conv_kernel.shape[0]
    length = extended.shape[0] - kernel_width + 1
    summed = conv_offset[None, :] + sum(
        (
            conv_kernel[offset][None, :] * extended[offset : offset + length]
            for offset in range(kernel_width)
        )
    )
    active = jax.nn.silu(summed)
    split_at = active.shape[1] - 2 * N
    step_size = jax.nn.softplus(raw_steps + step_bias[None, :])
    return (
        active[:, :split_at],
        active[:, split_at : split_at + N],
        active[:, split_at + N :],
        step_size,
        -jnp.exp(log_rates),
    )


def mix_out(x_conv, b_conv, c_conv, step_size, decay_rate, gate_in, skip_part, carried):
    length, head_count = step_size.shape
    x_heads = x_conv.reshape(length, head_count, -1)
    result = (
        ssd_scan(x_heads, step_size, decay_rate, b_conv, c_conv, carried)
        + skip_part[None, :, None] * x_heads
    )
    return result.reshape(length, -1) * jax.nn.silu(gate_in)


def rms_forward(values, gains):
    scaling = lax.rsqrt(jnp.mean(values * values, axis=-1, keepdims=True) + epsilon)
    return (values * scaling * gains[None, :], scaling)


def rms_backward(values, gains, scaling, upstream):
    weighted = upstream * gains[None, :]
    gain_grad = jnp.sum(upstream * values * scaling, axis=0)
    inner_mean = jnp.mean(weighted * values, axis=-1, keepdims=True)
    return (scaling * weighted - scaling**3 * values * inner_mean, gain_grad)


def contract(left, right, left_dim, right_dim):
    return lax.dot_general(
        left, right, (((left_dim,), (right_dim,)), ((), ())), preferred_element_type=jnp.float32
    )


def reorder(gradient, axis_pos, outer_count, inner_count):
    moved_axis = jnp.moveaxis(gradient, axis_pos, 0)
    regrouped = moved_axis.reshape((outer_count, inner_count, -1) + moved_axis.shape[1:])
    swapped = jnp.swapaxes(regrouped, 0, 1).reshape(moved_axis.shape)
    return jnp.moveaxis(swapped, 0, axis_pos)


def place_slice(part, total_len, start_at, axis_pos):
    zeros_shape = part.shape[:axis_pos] + (total_len,) + part.shape[axis_pos + 1 :]
    anchor = tuple((start_at if index_pos == axis_pos else 0 for index_pos in range(part.ndim)))
    return lax.dynamic_update_slice(jnp.zeros(zeros_shape, jnp.float32), part, anchor)


def shards(
    tokens,
    in_weight,
    step_weight,
    conv_kernel,
    conv_bias,
    step_bias,
    log_decay,
    skip_gain,
    gate_gain,
    norm_gain,
    out_weight,
    cotangent,
):
    gathered = (
        lax.all_gather(in_weight, "fsdp", axis=0, tiled=True),
        lax.all_gather(step_weight, "fsdp", axis=0, tiled=True),
        lax.all_gather(conv_kernel, "fsdp", axis=1, tiled=True),
        lax.all_gather(conv_bias, "fsdp", axis=0, tiled=True),
        lax.all_gather(step_bias, "fsdp", axis=0, tiled=True),
        lax.all_gather(log_decay, "fsdp", axis=0, tiled=True),
        lax.all_gather(skip_gain, "fsdp", axis=0, tiled=True),
        lax.all_gather(gate_gain, "fsdp", axis=0, tiled=True),
        lax.all_gather(norm_gain, "fsdp", axis=0, tiled=True),
        lax.all_gather(out_weight, "fsdp", axis=0, tiled=True),
    )
    w_in = gathered[0]
    w_step = gathered[1]
    w_out = gathered[9]
    kernel_f = gathered[2].astype(jnp.float32)
    bias_f = gathered[3].astype(jnp.float32)
    step_bias_f = gathered[4].astype(jnp.float32)
    decay_f = gathered[5].astype(jnp.float32)
    skip_f = gathered[6].astype(jnp.float32)
    gate_f = gathered[7].astype(jnp.float32)
    norm_f = gathered[8].astype(jnp.float32)
    inner_width = w_out.shape[0]
    head_count = w_step.shape[1]
    head_size = inner_width // head_count
    kernel_width = kernel_f.shape[0]
    out_cotangent = cotangent[0]
    residual = tokens[0].astype(jnp.float32)
    normed, scale_in = rms_forward(residual, norm_f)
    hidden = normed.astype(jnp.bfloat16)
    projected = jnp.dot(hidden, w_in, preferred_element_type=jnp.float32).astype(jnp.bfloat16)
    raw_steps = jnp.dot(hidden, w_step, preferred_element_type=jnp.float32).astype(jnp.bfloat16)
    seq_count = lax.axis_size("seq")
    position = lax.axis_index("seq")
    head_group = head_count // seq_count
    columns = head_group * head_size
    col_start = position * columns
    head_start = position * head_group
    tiled_bc = jnp.tile(projected[:, 2 * inner_width :], (1, seq_count))
    gate_part, x_part, step_part, bc_part = (
        lax.all_to_all(projected[:, :inner_width], "seq", split_axis=1, concat_axis=0, tiled=True),
        lax.all_to_all(
            projected[:, inner_width : 2 * inner_width],
            "seq",
            split_axis=1,
            concat_axis=0,
            tiled=True,
        ),
        lax.all_to_all(raw_steps, "seq", split_axis=1, concat_axis=0, tiled=True),
        lax.all_to_all(tiled_bc, "seq", split_axis=1, concat_axis=0, tiled=True),
    )
    my_kernel = jnp.concatenate(
        [lax.dynamic_slice_in_dim(kernel_f, col_start, columns, 1), kernel_f[:, inner_width:]],
        axis=1,
    )
    my_bias = jnp.concatenate(
        [lax.dynamic_slice_in_dim(bias_f, col_start, columns, 0), bias_f[inner_width:]], axis=0
    )
    my_step_bias = lax.dynamic_slice_in_dim(step_bias_f, head_start, head_group, 0)
    my_decay = lax.dynamic_slice_in_dim(decay_f, head_start, head_group, 0)
    my_skip = lax.dynamic_slice_in_dim(skip_f, head_start, head_group, 0)
    padding = jnp.zeros((kernel_width - 1, columns + 2 * N), jnp.float32)
    extended = jnp.concatenate(
        [padding, jnp.concatenate([x_part, bc_part], axis=1).astype(jnp.float32)], axis=0
    )
    prepared, pull_prepare = jax.vjp(
        prepare, extended, step_part.astype(jnp.float32), my_kernel, my_bias, my_step_bias, my_decay
    )
    x_conv, b_conv, c_conv, step_size, decay_rate = prepared
    start_state = jnp.zeros((head_group, head_size, N), jnp.float32)
    gated_f, pull_mix = jax.vjp(
        mix_out,
        x_conv,
        b_conv,
        c_conv,
        step_size,
        decay_rate,
        gate_part.astype(jnp.float32),
        my_skip,
        start_state,
    )
    gated_out = lax.all_to_all(
        gated_f.astype(jnp.bfloat16), "seq", split_axis=0, concat_axis=1, tiled=True
    )
    gated_back = gated_out.astype(jnp.float32)
    mixed_f, scale_out = rms_forward(gated_back, gate_f)
    mixed_norm = mixed_f.astype(jnp.bfloat16)
    block_out = (residual + jnp.dot(mixed_norm, w_out, preferred_element_type=jnp.float32)).astype(
        jnp.bfloat16
    )
    out_grad = contract(mixed_norm, out_cotangent, 0, 0)
    mixed_grad = contract(out_cotangent, w_out, 1, 1)
    gated_grad, gate_gain_grad = rms_backward(gated_back, gate_f, scale_out, mixed_grad)
    gated_grad_b = lax.optimization_barrier(gated_grad.astype(jnp.bfloat16))
    gated_grad_h = lax.all_to_all(
        gated_grad_b, "seq", split_axis=1, concat_axis=0, tiled=True
    ).astype(jnp.float32)
    x_grad, b_grad, c_grad, step_grad, rate_grad, gate_in_grad, skip_grad_h, unused = pull_mix(
        gated_grad_h
    )
    ext_grad, raw_grad, kernel_grad_h, bias_grad_h, step_bias_grad_h, decay_grad_h = pull_prepare(
        (x_grad, b_grad, c_grad, step_grad, rate_grad)
    )
    body_grad = ext_grad[kernel_width - 1 :]
    gate_back, x_back, step_back = (
        lax.all_to_all(
            gate_in_grad.astype(jnp.bfloat16), "seq", split_axis=0, concat_axis=1, tiled=True
        ),
        lax.all_to_all(
            body_grad[:, :columns].astype(jnp.bfloat16),
            "seq",
            split_axis=0,
            concat_axis=1,
            tiled=True,
        ),
        lax.all_to_all(
            raw_grad.astype(jnp.bfloat16), "seq", split_axis=0, concat_axis=1, tiled=True
        ),
    )
    bc_back = lax.psum_scatter(
        body_grad[:, columns:].astype(jnp.bfloat16), "seq", scatter_dimension=0, tiled=True
    )
    proj_grad = jnp.concatenate([gate_back, x_back, bc_back], axis=1)
    kernel_grad = jnp.concatenate(
        [
            place_slice(kernel_grad_h[:, :columns], inner_width, col_start, 1),
            kernel_grad_h[:, columns:],
        ],
        axis=1,
    )
    bias_grad = jnp.concatenate(
        [place_slice(bias_grad_h[:columns], inner_width, col_start, 0), bias_grad_h[columns:]],
        axis=0,
    )
    step_bias_grad = place_slice(step_bias_grad_h, head_count, head_start, 0)
    decay_grad = place_slice(decay_grad_h, head_count, head_start, 0)
    skip_grad = place_slice(skip_grad_h, head_count, head_start, 0)
    in_grad = contract(hidden, proj_grad, 0, 0)
    step_w_grad = contract(hidden, step_back, 0, 0)
    hidden_grad = contract(proj_grad, w_in, 1, 1) + contract(step_back, w_step, 1, 1)
    resid_grad, norm_gain_grad = rms_backward(residual, norm_f, scale_in, hidden_grad)
    input_grad = out_cotangent.astype(jnp.float32) + resid_grad
    fsdp_count = lax.axis_size("fsdp")
    seq_total = lax.axis_size("seq")

    def spread_heads(gradient):
        return jnp.tile(gradient.reshape(fsdp_count, -1), (seq_total, 1)).reshape(-1)

    blocks = (
        lax.psum_scatter(
            reorder(in_grad, 0, fsdp_count, seq_total),
            ("seq", "fsdp"),
            scatter_dimension=0,
            tiled=True,
        ),
        lax.psum_scatter(
            reorder(step_w_grad, 0, fsdp_count, seq_total),
            ("seq", "fsdp"),
            scatter_dimension=0,
            tiled=True,
        ),
        lax.psum_scatter(
            reorder(kernel_grad, 1, fsdp_count, seq_total),
            ("seq", "fsdp"),
            scatter_dimension=1,
            tiled=True,
        ),
        lax.psum_scatter(
            reorder(bias_grad, 0, fsdp_count, seq_total),
            ("seq", "fsdp"),
            scatter_dimension=0,
            tiled=True,
        ),
        lax.psum_scatter(
            spread_heads(step_bias_grad), ("seq", "fsdp"), scatter_dimension=0, tiled=True
        ),
        lax.psum_scatter(
            spread_heads(decay_grad), ("seq", "fsdp"), scatter_dimension=0, tiled=True
        ),
        lax.psum_scatter(spread_heads(skip_grad), ("seq", "fsdp"), scatter_dimension=0, tiled=True),
        lax.psum_scatter(
            reorder(gate_gain_grad, 0, fsdp_count, seq_total),
            ("seq", "fsdp"),
            scatter_dimension=0,
            tiled=True,
        ),
        lax.psum_scatter(
            reorder(norm_gain_grad, 0, fsdp_count, seq_total),
            ("seq", "fsdp"),
            scatter_dimension=0,
            tiled=True,
        ),
        lax.psum_scatter(
            reorder(out_grad, 0, fsdp_count, seq_total),
            ("seq", "fsdp"),
            scatter_dimension=0,
            tiled=True,
        ),
    )
    joined = (
        lax.all_gather(blocks[0], "seq", axis=0, tiled=True),
        lax.all_gather(blocks[1], "seq", axis=0, tiled=True),
        lax.all_gather(blocks[2], "seq", axis=1, tiled=True),
        lax.all_gather(blocks[3], "seq", axis=0, tiled=True),
        lax.all_gather(blocks[7], "seq", axis=0, tiled=True),
        lax.all_gather(blocks[8], "seq", axis=0, tiled=True),
        lax.all_gather(blocks[9], "seq", axis=0, tiled=True),
    )
    totals = (
        joined[0],
        joined[1],
        joined[2],
        joined[3],
        blocks[4],
        blocks[5],
        blocks[6],
        joined[4],
        joined[5],
        joined[6],
    )
    return (
        block_out[None],
        input_grad[None],
        totals[0],
        totals[1],
        totals[2],
        totals[3],
        totals[4],
        totals[5],
        totals[6],
        totals[7],
        totals[8],
        totals[9],
    )


def solution(mesh):
    placed = (
        P("fsdp", "seq", None),
        P("fsdp", None),
        P("fsdp", None),
        P(None, "fsdp"),
        P("fsdp"),
        P("fsdp"),
        P("fsdp"),
        P("fsdp"),
        P("fsdp"),
        P("fsdp"),
        P("fsdp", None),
        P("fsdp", "seq", None),
    )
    return jax.shard_map(
        shards,
        mesh=mesh,
        in_specs=placed,
        out_specs=(
            P("fsdp", "seq", None),
            P("fsdp", "seq", None),
            P("fsdp", None),
            P("fsdp", None),
            P(None, "fsdp"),
            P("fsdp"),
            P("fsdp"),
            P("fsdp"),
            P("fsdp"),
            P("fsdp"),
            P("fsdp"),
            P("fsdp", None),
        ),
        check_vma=False,
    )
```

profile of v0, /device:TPU:0, one launch (start us, length us, event | category | flops | bytes accessed | tf_op | source)
XLA Modules:
  0.0 1683.6 jit_solution(14580512450812876870)
XLA Ops:
  28.3 108.3 %all-gather.9.cloned.1.call-done = bf16[1536,6400]{1,0:T(8,128)(2,1)} async-done(((bf16[384,6400]{1,0:T(8,128)(2,1)}), bf16[1536,6400]{1,0:T(8,128)(2,1)}) %all-gather.9.cloned.1.call-update) | async-done | bytes 19660816 | tf_op jit(solution)/shard_map/all_gather | solution.py:126
  154.5 12.8 all-to-all-done.2
  211.3 74.2 %while.41 = (s32[]{:T(128)}, f32[6,64,128]{2,1,0:T(8,128)S(1)}, f32[4,256,6,64]{1,0,3,2:T(4,128)}, f32[4,6,64,128]{3,2,1,0:T(8,128)}, f32[4,256,6]{1,2,0:T(8,128...) while((s32[]{:T(128)}, f32[6,64,128]{2,1,0:T(8,128)S(1)}, ...), condition=%wide.region_4.5_spmd.clone, body=%wide.region_1.4_spmd.clone.sunk | while | flops 706957824 | bytes 5773208 | solution.py:45
  310.4 14.1 all-to-all-done.4
  346.8 14.6 all-to-all-done.5
  376.5 167.4 %while.42 = (s32[]{:T(128)}, f32[6]{0:T(128)}, f32[6,64,128]{2,1,0:T(8,128)S(1)}, f32[4,256,6,64]{1,0,3,2:T(4,128)}, f32[4,256,6]{1,2,0:T(8,128)}, /*index=5*/f3...) while((s32[]{:T(128)}, f32[6]{0:T(128)}, ...), condition=%wide.region_20.21_spmd.clone, body=%wide.region_7.20_spmd.clone.sunk | while | flops 1669247488 | bytes 18030544 | solution.py:45
  402.7 9.5 dynamic_update_slice.93
  444.6 9.5 dynamic_update_slice.93
  528.3 9.5 dynamic_update_slice.93
  575.7 9.9 all_to_all.141
  595.2 13.1 all-to-all-done.6
  613.6 21.0 %all-to-all-done.7 = bf16[8,128,384]{2,1,0:T(8,128)(2,1)} async-done(((bf16[8,128,384]{2,1,0:T(8,128)(2,1)}), bf16[8,128,384]{2,1,0:T(8,128)(2,1)}, u32[]{:S(2)}, u32[]{:S(2)}) %all-to-all-start.7) | async-done | bytes 786464 | tf_op jit(solution)/shard_map/all_to_all | solution.py:233
  639.3 12.3 fusion.152
  653.8 20.1 %convolution_bitcast_fusion.2 = f32[8,4,48,6400]{3,2,0,1:T(8,128)} fusion(bf16[4,8,48,128]{3,2,1,0:T(8,128)(2,1)S(1)} %bitcast.577, bf16[128,6400]{1,0:T(8,128)(2,1)} %constant_dynamic-update-slice_fusion), kind=kOutput, calls=%fused_computation.128 | convolution fusion | flops 2516582400 | bytes 41353216 | tf_op jit(solution)/shard_map/dot_general | solution.py:93
  673.9 28.6 %copy.323 = f32[8,4,48,6400]{3,2,1,0:T(8,128)} copy(f32[8,4,48,6400]{3,2,0,1:T(8,128)} %convolution_bitcast_fusion.2) | data formatting | bytes 78643200 | tf_op jit(solution)/shard_map/transpose | solution.py:101
  711.7 130.3 %reduce-scatter.12.cloned.1.call-done = f32[96,1536]{1,0:T(8,128)} async-done(((f32[3072,1536]{1,0:T(8,128)}), f32[96,1536]{1,0:T(8,128)}) %reduce-scatter.12.cloned.1.call-update) | async-done | bytes 589840 | tf_op jit(solution)/shard_map/reduce_scatter | solution.py:317
  842.1 364.2 %reduce-scatter.10.cloned.1.call-done = f32[48,6400]{1,0:T(8,128)} async-done(((f32[1536,6400]{1,0:T(8,128)}), f32[48,6400]{1,0:T(8,128)}) %reduce-scatter.10.cloned.1.call-update) | async-done | bytes 1228816 | tf_op jit(solution)/shard_map/reduce_scatter | solution.py:274
  1214.8 123.9 %all-reduce.33.cloned.1.call-done = (f32[4,3328]{1,0:T(4,128)}, f32[3328]{0:T(1024)}, f32[384]{0:T(512)}, f32[384]{0:T(512)}, f32[384]{0:T(512)}, /*index=5*/f32[3072]{0:T(1024)}, f32[1536]{0:T(1024)}) async-done(((f32[4,3328]{1,0:T(4,128)}, f32[3328]{0:T(1024)}, f32[384]{0:T(512)}, f32[384]{0:T(512)}, f32[384]{0:T(512)}, /*index=5*/f32[3072]{0:T(1024)}, f32[1536]{0:T(1024)}), (f32[4,3328]{1,0:T(4,128)}, ...) | async-done | bytes 89616
  1339.5 27.0 %all-gather.3 = f32[8,104,4]{1,2,0:T(4,128)S(1)} all-gather(f32[1,104,4]{1,2,0:T(4,128)S(1)} %dynamic-slice_bitcast_fusion.7), channel_id=1, replica_groups=mesh['seq'=8,'fsdp'=4] {'seq'}, dimensions={0}, use_global_device_ids=true | all-gather | bytes 14976 | tf_op jit(solution)/shard_map/all_gather | solution.py:327
  1373.5 35.5 %all-reduce.29 = (f32[832]{0:T(1024)}, f32[768]{0:T(1024)}, f32[384]{0:T(512)}) all-reduce(f32[832]{0:T(1024)S(1)} %dynamic-slice_dynamic-update-slice_fusion.2, f32[768]{0:T(1024)S(1)} %dynamic-slice_dynamic-update-slice_fusion.1, f32[384]{0:T(512)S(1)} %dynamic-slice_dynamic-update-slice_fusion), channel_id=1, replica_groups=mesh['seq'=8,'fsdp'=4] {'seq'}, use_global_device_ids=true, to_apply=%add.18 | all-reduce | flops 1984 | bytes 15872
  1409.1 32.7 %reduce-scatter.14.cloned.1.call-done = f32[48,48]{1,0:T(8,128)} async-done(((f32[1536,48]{1,0:T(8,128)}), f32[48,48]{1,0:T(8,128)}) %reduce-scatter.14.cloned.1.call-update) | async-done | bytes 9232 | tf_op jit(solution)/shard_map/reduce_scatter | solution.py:280
  1441.8 32.1 %all_gather.62 = f32[384,48]{1,0:T(8,128)S(1)} all-gather(f32[48,48]{1,0:T(8,128)} %reduce-scatter.14.cloned.1.call-done), channel_id=1, replica_groups=mesh['seq'=8,'fsdp'=4] {'seq'}, dimensions={0}, use_global_device_ids=true | all-gather | bytes 82944 | tf_op jit(solution)/shard_map/all_gather | solution.py:326
  1474.6 48.8 %all-gather.15.cloned.1.call-done = f32[768,1536]{1,0:T(8,128)} async-done(((f32[96,1536]{1,0:T(8,128)}), f32[768,1536]{1,0:T(8,128)}) %all-gather.15.cloned.1.call-update) | async-done | bytes 4718608 | tf_op jit(solution)/shard_map/all_gather | solution.py:331
  1523.4 142.8 %all-gather.13.cloned.1.call-done = f32[384,6400]{1,0:T(8,128)} async-done(((f32[48,6400]{1,0:T(8,128)}), f32[384,6400]{1,0:T(8,128)}) %all-gather.13.cloned.1.call-update) | async-done | bytes 9830416 | tf_op jit(solution)/shard_map/all_gather | solution.py:325
  (656 shorter events, 442.9 us)
Async XLA Ops:
  7.2 129.5 %all-gather.9.cloned.1.call-start = ((), (), s32[]{:S(2)}) async-start(), calls=%async_computation.13 | async-start | bytes 24576000 | tf_op jit(solution)/shard_map/all_gather | solution.py:126
  14.2 122.5 %copy-start.41 = (f32[1536]{0:T(1024)}, f32[1536]{0:T(1024)S(1)}, u32[]{:S(2)}) copy-start(f32[1536]{0:T(1024)S(1)} %reshape.548) | copy-start | bytes 18436
  20.7 116.0 %copy-start.58 = (f32[128]{0:T(128)}, f32[128]{0:T(128)S(1)}, u32[]{:S(2)}) copy-start(f32[128]{0:T(128)S(1)} %get-tuple-element.798) | copy-start | bytes 1540
  21.6 124.5 %all-to-all-start = ((bf16[128,8,6]{0,2,1:T(8,128)(2,1)}), bf16[128,8,6]{0,2,1:T(8,128)(2,1)S(1)}, u32[]{:S(2)}, u32[]{:S(2)}) async-start(bf16[128,8,6]{0,2,1:T(8,128)(2,1)} %all_to_all.106), calls=%async_computation | async-start | bytes 32768 | tf_op jit(solution)/shard_map/all_to_all | solution.py:173
  27.6 297.5 %all-gather.11.cloned.1.call-start = ((), (), s32[]{:S(2)}) async-start(), calls=%async_computation.14 | async-start | bytes 11796480 | tf_op jit(solution)/shard_map/all_gather | solution.py:135
  146.9 20.4 %all-to-all-start.2 = ((bf16[128,8,256]{2,0,1:T(8,128)(2,1)}), bf16[128,8,256]{2,0,1:T(8,128)(2,1)S(1)}, u32[]{:S(2)}, u32[]{:S(2)}) async-start(bf16[128,8,256]{2,0,1:T(8,128)(2,1)} %tile.28), calls=%async_computation.2 | async-start | bytes 1048576 | tf_op jit(solution)/shard_map/all_to_all | solution.py:174
  167.4 24.0 %all-to-all-start.1 = ((bf16[128,8,384]{2,0,1:T(8,128)(2,1)}), bf16[128,8,384]{2,0,1:T(8,128)(2,1)S(1)}, u32[]{:S(2)}, u32[]{:S(2)}) async-start(bf16[128,8,384]{2,0,1:T(8,128)(2,1)} %bitcast.418), calls=%async_computation.1 | async-start | bytes 1572864 | tf_op jit(solution)/shard_map/all_to_all | solution.py:166
  181.1 160.6 %copy-start.68 = (f32[48]{0:T(128)}, f32[48]{0:T(128)S(1)}, u32[]{:S(2)}) copy-start(f32[48]{0:T(128)S(1)} %convert_element_type.138) | copy-start | bytes 580
  187.1 108.4 %copy-start.55 = (f32[384]{0:T(512)}, f32[384]{0:T(512)S(1)}, u32[]{:S(2)}) copy-start(f32[384]{0:T(512)S(1)} %mul.640) | copy-start | bytes 4612
  191.4 99.3 %all-to-all-start.3 = ((bf16[128,8,384]{0,2,1:T(8,128)(2,1)}), bf16[128,8,384]{0,2,1:T(8,128)(2,1)}, u32[]{:S(2)}, u32[]{:S(2)}) async-start(bf16[128,8,384]{0,2,1:T(8,128)(2,1)} %bitcast.18), calls=%async_computation.3 | async-start | bytes 1572864 | tf_op jit(solution)/shard_map/all_to_all | solution.py:165
  298.9 25.6 %all-to-all-start.4 = ((bf16[8,128,384]{2,1,0:T(8,128)(2,1)}), bf16[8,128,384]{2,1,0:T(8,128)(2,1)S(1)}, u32[]{:S(2)}, u32[]{:S(2)}) async-start(bf16[8,128,384]{2,1,0:T(8,128)(2,1)} %bitcast.580), calls=%async_computation.4 | async-start | bytes 1572864 | tf_op jit(solution)/shard_map/all_to_all | solution.py:206
  337.4 24.1 %all-to-all-start.5 = ((bf16[128,8,384]{0,2,1:T(8,128)(2,1)}), bf16[128,8,384]{0,2,1:T(8,128)(2,1)}, u32[]{:S(2)}, u32[]{:S(2)}) async-start(bf16[128,8,384]{0,2,1:T(8,128)(2,1)} %bitcast.583), calls=%async_computation.5 | async-start | bytes 1572864 | tf_op jit(solution)/shard_map/all_to_all | solution.py:219
  341.6 296.2 %reduce-scatter.8.cloned.1.call-start = ((), (), s32[]{:S(2)}) async-start(), calls=%async_computation.15 | async-start | bytes 589824 | tf_op jit(solution)/shard_map/reduce_scatter | solution.py:244
  563.5 278.5 %reduce-scatter.12.cloned.1.call-start = ((), (), s32[]{:S(2)}) async-start(), calls=%async_computation.18 | async-start | bytes 19464192 | tf_op jit(solution)/shard_map/reduce_scatter | solution.py:317
  585.6 22.7 %all-to-all-start.6 = ((bf16[8,128,384]{2,1,0:T(8,128)(2,1)}), bf16[8,128,384]{2,1,0:T(8,128)(2,1)S(1)}, u32[]{:S(2)}, u32[]{:S(2)}) async-start(bf16[8,128,384]{2,1,0:T(8,128)(2,1)} %bitcast.29), calls=%async_computation.6 | async-start | bytes 1572864 | tf_op jit(solution)/shard_map/all_to_all | solution.py:230
  608.3 26.4 %all-to-all-start.7 = ((bf16[8,128,384]{2,1,0:T(8,128)(2,1)}), bf16[8,128,384]{2,1,0:T(8,128)(2,1)}, u32[]{:S(2)}, u32[]{:S(2)}) async-start(bf16[8,128,384]{2,1,0:T(8,128)(2,1)} %bitcast.584), calls=%async_computation.7 | async-start | bytes 1572864 | tf_op jit(solution)/shard_map/all_to_all | solution.py:233
  612.5 593.8 %reduce-scatter.10.cloned.1.call-start = ((), (), s32[]{:S(2)}) async-start(), calls=%async_computation.16 | async-start | bytes 40550400 | tf_op jit(solution)/shard_map/reduce_scatter | solution.py:274
  702.5 636.2 %all-reduce.33.cloned.1.call-start = ((), (), s32[]{:S(2)}) async-start(), calls=%async_computation.21 | async-start | bytes 192512
  710.4 731.4 %reduce-scatter.14.cloned.1.call-start = ((), (), s32[]{:S(2)}) async-start(), calls=%async_computation.20 | async-start | bytes 811008 | tf_op jit(solution)/shard_map/reduce_scatter | solution.py:280
  711.6 494.7 %copy-start.74 = (u32[32]{0:T(128)S(1)}, u32[32]{0:T(128)}, u32[]{:S(2)}) copy-start(u32[32]{0:T(128)} %constant.200) | copy-start | bytes 388
  711.6 497.3 %copy-start.36 = (f32[4,1,768]{2,1,0:T(1,128)S(1)}, f32[4,1,768]{2,1,0:T(1,128)}, u32[]{:S(2)}) copy-start(f32[4,1,768]{2,1,0:T(1,128)} %copy-done.35) | copy-start | bytes 36868
  711.6 497.3 %copy-start.61 = (f32[128]{0:T(128)S(1)}, f32[128]{0:T(128)}, u32[]{:S(2)}) copy-start(f32[128]{0:T(128)} %copy-done.60) | copy-start | bytes 1540
  711.7 811.7 %all-gather.15.cloned.1.call-start = ((), (), s32[]{:S(2)}) async-start(), calls=%async_computation.19 | async-start | bytes 5308416 | tf_op jit(solution)/shard_map/all_gather | solution.py:331
  842.1 824.1 %all-gather.13.cloned.1.call-start = ((), (), s32[]{:S(2)}) async-start(), calls=%async_computation.17 | async-start | bytes 11059200 | tf_op jit(solution)/shard_map/all_gather | solution.py:325
  (87 other events, 676.3 us)
Sparse Core Ops, SparseCore 0:
  9.6 127.0 all-gather.8
  138.2 64.7 all-gather.10
  563.6 63.3 reduce-scatter.7
  633.3 208.7 reduce-scatter.11
  848.3 357.9 reduce-scatter.9
  1213.8 124.8 all-reduce.32
  1344.4 97.3 reduce-scatter.13
  1444.0 79.3 all-gather.14
  1525.6 140.5 all-gather.12
where the time goes:
time: 1690 us; the launch traced here: 1680 us
  waiting for transfers between devices  1030 us (61%)
  local copies, waits for them, and re-layouts  232 us (14%)
  blocking collectives  135 us (8%)
  matrix products  132 us (8%)
  other arithmetic  96 us (6%)
  starting transfers between devices  38.3 us (2%)
  between operations  18.4 us (1%)
    reduce_scatter x1, waiting for transfers between devices, shards(): lax.psum_scatter(reorder(in_grad, 0, fsdp_count, seq_total), ('seq', 'fsd...  364 us
    all_gather x1, waiting for transfers between devices, shards(): lax.all_gather(blocks[0], 'seq', axis=0, tiled=True)  143 us
    reduce_scatter x1, waiting for transfers between devices, shards(): lax.psum_scatter(reorder(out_grad, 0, fsdp_count, seq_total), ('seq', 'fs...  130 us
    unnamed x10, waiting for transfers between devices  125 us
    all_gather x1, waiting for transfers between devices, shards(): lax.all_gather(in_weight, 'fsdp', axis=0, tiled=True)  108 us
    dynamic_update_slice x16, local copies, waits for them, and re-layouts, ssd_scan(): finals, outputs = lax.scan(jax.checkpoint(advance), carried, pieces)  79.5 us
    another operation x33, other arithmetic  50.7 us
    all_gather x1, waiting for transfers between devices, shards(): lax.all_gather(blocks[9], 'seq', axis=0, tiled=True)  48.8 us
  transfers between devices with their start and end apart: 17, of which 13 were waited for; matrix products, arithmetic and copies ran while one was open for 14% of the time, Pallas kernels for 0%

commit v1 on v0

--- a/solution.py
+++ b/solution.py
@@ -7,6 +7,27 @@
 BLOCK = 256
 epsilon = 1e-05
 highest = lax.Precision.HIGHEST
+
+
+def laid_out(blocks, dim):
+    blocks = jnp.moveaxis(blocks, 0, dim)
+    dims = blocks.shape
+    return blocks.reshape(*dims[:dim], dims[dim] * dims[dim + 1], *dims[dim + 2 :])
+
+
+def doubled(shard, axis):
+    peers, index = (lax.axis_size(axis), lax.axis_index(axis))
+    parts, distance = (shard[None], 1)
+    while distance < peers:
+        received = lax.ppermute(parts, axis, [(i, i ^ distance) for i in range(peers)])
+        low = index & distance == 0
+        parts = jnp.concatenate([jnp.where(low, parts, received), jnp.where(low, received, parts)])
+        distance *= 2
+    return parts
+
+
+def gather_by_bits(array, axis, dim):
+    return laid_out(doubled(array, axis), dim)
 
 
 def block_step(carried, pieces, decay_rate):
@@ -123,7 +144,7 @@
     cotangent,
 ):
     gathered = (
-        lax.all_gather(in_weight, "fsdp", axis=0, tiled=True),
+        gather_by_bits(in_weight, "fsdp", 0),
         lax.all_gather(step_weight, "fsdp", axis=0, tiled=True),
         lax.all_gather(conv_kernel, "fsdp", axis=1, tiled=True),
         lax.all_gather(conv_bias, "fsdp", axis=0, tiled=True),

time: 1690 us -> 1910 us (1.13)
  blocking collectives: 135 us -> 391 us
  waiting for transfers between devices: 1030 us -> 929 us
  other arithmetic: 96 us -> 140 us
    all_gather x1, blocking collectives: 6.18 us -> 263 us  [shards(): lax.all_gather(norm_gain, 'fsdp', axis=0, tiled=True)]
    all_gather x1 -> x0, waiting for transfers between devices: 108 us -> none  [shards(): lax.all_gather(in_weight, 'fsdp', axis=0, tiled=True)]
    select_n x0 -> x2, other arithmetic: none -> 19.9 us  [doubled(): jnp.where(low, parts, received)]
    unnamed x173 -> x171, local copies, waits for them, and re-layouts: 41.2 us -> 42.9 us
    unnamed x10 -> x9, waiting for transfers between devices: 125 us -> 124 us
  transfers between devices with their start and end apart: 17 -> 18, of which waited for: 13 -> 13; matrix products, arithmetic and copies ran while one was open for 14% -> 14% of each run, Pallas kernels for 0% -> 0%
where the time goes in v1:
time: 1910 us; the launch traced here: 1900 us
  waiting for transfers between devices  929 us (49%)
  blocking collectives  391 us (20%)
  local copies, waits for them, and re-layouts  239 us (13%)
  other arithmetic  140 us (7%)
  matrix products  135 us (7%)
  starting transfers between devices  41.2 us (2%)
    reduce_scatter x1, waiting for transfers between devices, shards(): lax.psum_scatter(reorder(in_grad, 0, fsdp_count, seq_total), ('seq', 'fsd...  364 us
    all_gather x1, blocking collectives, shards(): lax.all_gather(norm_gain, 'fsdp', axis=0, tiled=True)  263 us
    all_gather x1, waiting for transfers between devices, shards(): lax.all_gather(blocks[0], 'seq', axis=0, tiled=True)  143 us
    reduce_scatter x1, waiting for transfers between devices, shards(): lax.psum_scatter(reorder(out_grad, 0, fsdp_count, seq_total), ('seq', 'fs...  131 us
    unnamed x9, waiting for transfers between devices  124 us
    dynamic_update_slice x16, local copies, waits for them, and re-layouts, ssd_scan(): finals, outputs = lax.scan(jax.checkpoint(advance), carried, pieces)  79.4 us
    another operation x33, other arithmetic  53.5 us
    all_gather x1, waiting for transfers between devices, shards(): lax.all_gather(blocks[9], 'seq', axis=0, tiled=True)  48.8 us
  transfers between devices with their start and end apart: 18, of which 13 were waited for; matrix products, arithmetic and copies ran while one was open for 14% of the time, Pallas kernels for 0%

profile of v1, /device:TPU:0, one launch (start us, length us, event | category | flops | bytes accessed | tf_op | source)
XLA Modules:
  0.0 1895.1 jit_solution(5513493673933471757)
XLA Ops:
  35.8 263.3 %all-gather = bf16[4,1,384]{2,1,0:T(2,128)(2,1)S(1)} all-gather(bf16[1,1,384]{2,1,0:T(2,128)(2,1)S(1)} %reshape.558), channel_id=1, replica_groups=mesh['seq'=8,'fsdp'=4] {'fsdp'}, dimensions={0}, use_global_device_ids=true | all-gather | bytes 3840 | tf_op jit(solution)/shard_map/all_gather | solution.py:155
  312.4 11.6 broadcast_select_fusion.3
  346.2 13.3 all-to-all-done.2
  403.6 87.3 %while.41 = (s32[]{:T(128)}, f32[6,64,128]{2,1,0:T(8,128)S(1)}, f32[4,256,6,64]{1,0,3,2:T(4,128)}, f32[4,6,64,128]{3,2,1,0:T(8,128)}, f32[4,256,6]{1,2,0:T(8,128...) while((s32[]{:T(128)}, f32[6,64,128]{2,1,0:T(8,128)S(1)}, ...), condition=%wide.region_4.5_spmd.clone, body=%wide.region_1.4_spmd.clone.sunk | while | flops 706957824 | bytes 5768624 | solution.py:66
  415.9 9.5 dynamic_update_slice.89
  437.7 9.5 dynamic_update_slice.89
  517.2 13.7 all-to-all-done.4
  553.2 14.6 all-to-all-done.5
  582.8 171.7 %while.42 = (s32[]{:T(128)}, f32[6]{0:T(128)}, f32[6,64,128]{2,1,0:T(8,128)}, f32[4,256,6,64]{1,0,3,2:T(4,128)}, f32[4,256,6]{1,2,0:T(8,128)}, /*index=5*/f32[4,...) while((s32[]{:T(128)}, f32[6]{0:T(128)}, ...), condition=%wide.region_20.21_spmd.clone, body=%wide.region_7.20_spmd.clone.sunk | while | flops 1669247488 | bytes 17047420 | solution.py:66
  786.4 10.0 all_to_all.141
  805.9 13.2 all-to-all-done.6
  825.0 20.2 %all-to-all-done.7 = bf16[8,128,384]{2,1,0:T(8,128)(2,1)S(1)} async-done(((bf16[8,128,384]{2,1,0:T(8,128)(2,1)}), bf16[8,128,384]{2,1,0:T(8,128)(2,1)S(1)}, u32[]{:S(2)}, u32[]{:S(2)}) %all-to-all-start.7) | async-done | bytes 786464 | tf_op jit(solution)/shard_map/all_to_all | solution.py:254
  847.4 13.8 fusion.121
  864.7 19.5 %convolution_bitcast_fusion.2 = f32[8,4,48,6400]{3,2,0,1:T(8,128)} fusion(bf16[4,8,48,128]{3,2,1,0:T(8,128)(2,1)} %bitcast.610, bf16[128,6400]{1,0:T(8,128)(2,1)S(1)} %constant_dynamic-update-slice_fusion), kind=kOutput, calls=%fused_computation.129 | convolution fusion | flops 2516582400 | bytes 41353216 | tf_op jit(solution)/shard_map/dot_general | solution.py:114
  884.2 28.5 %copy.323 = f32[8,4,48,6400]{3,2,1,0:T(8,128)} copy(f32[8,4,48,6400]{3,2,0,1:T(8,128)} %convolution_bitcast_fusion.2) | data formatting | bytes 78643200 | tf_op jit(solution)/shard_map/transpose | solution.py:122
  922.0 131.4 %reduce-scatter.12.cloned.1.call-done = f32[96,1536]{1,0:T(8,128)} async-done(((f32[3072,1536]{1,0:T(8,128)}), f32[96,1536]{1,0:T(8,128)}) %reduce-scatter.12.cloned.1.call-update) | async-done | bytes 589840 | tf_op jit(solution)/shard_map/reduce_scatter | solution.py:338
  1053.5 364.0 %reduce-scatter.10.cloned.1.call-done = f32[48,6400]{1,0:T(8,128)} async-done(((f32[1536,6400]{1,0:T(8,128)}), f32[48,6400]{1,0:T(8,128)}) %reduce-scatter.10.cloned.1.call-update) | async-done | bytes 1228816 | tf_op jit(solution)/shard_map/reduce_scatter | solution.py:295
  1426.0 123.8 %all-reduce.33.cloned.1.call-done = (f32[4,3328]{1,0:T(4,128)}, f32[3328]{0:T(1024)}, f32[384]{0:T(512)}, f32[384]{0:T(512)}, f32[384]{0:T(512)}, /*index=5*/f32[3072]{0:T(1024)}, f32[1536]{0:T(1024)}) async-done(((f32[4,3328]{1,0:T(4,128)}, f32[3328]{0:T(1024)}, f32[384]{0:T(512)}, f32[384]{0:T(512)}, f32[384]{0:T(512)}, /*index=5*/f32[3072]{0:T(1024)}, f32[1536]{0:T(1024)}), (f32[4,3328]{1,0:T(4,128)}, ...) | async-done | bytes 89616
  1550.6 27.0 %all-gather.3 = f32[8,104,4]{1,2,0:T(4,128)S(1)} all-gather(f32[1,104,4]{1,2,0:T(4,128)S(1)} %dynamic-slice_bitcast_fusion.7), channel_id=1, replica_groups=mesh['seq'=8,'fsdp'=4] {'seq'}, dimensions={0}, use_global_device_ids=true | all-gather | bytes 14976 | tf_op jit(solution)/shard_map/all_gather | solution.py:348
  1584.6 35.6 %all-reduce.29 = (f32[832]{0:T(1024)}, f32[768]{0:T(1024)}, f32[384]{0:T(512)}) all-reduce(f32[832]{0:T(1024)S(1)} %dynamic-slice_dynamic-update-slice_fusion.2, f32[768]{0:T(1024)S(1)} %dynamic-slice_dynamic-update-slice_fusion.1, f32[384]{0:T(512)S(1)} %dynamic-slice_dynamic-update-slice_fusion), channel_id=1, replica_groups=mesh['seq'=8,'fsdp'=4] {'seq'}, use_global_device_ids=true, to_apply=%add.18 | all-reduce | flops 1984 | bytes 15872
  1620.2 32.6 %reduce-scatter.14.cloned.1.call-done = f32[48,48]{1,0:T(8,128)} async-done(((f32[1536,48]{1,0:T(8,128)}), f32[48,48]{1,0:T(8,128)}) %reduce-scatter.14.cloned.1.call-update) | async-done | bytes 9232 | tf_op jit(solution)/shard_map/reduce_scatter | solution.py:301
  1652.8 32.1 %all_gather.58 = f32[384,48]{1,0:T(8,128)S(1)} all-gather(f32[48,48]{1,0:T(8,128)} %reduce-scatter.14.cloned.1.call-done), channel_id=1, replica_groups=mesh['seq'=8,'fsdp'=4] {'seq'}, dimensions={0}, use_global_device_ids=true | all-gather | bytes 82944 | tf_op jit(solution)/shard_map/all_gather | solution.py:347
  1685.6 48.8 %all-gather.12.cloned.1.call-done = f32[768,1536]{1,0:T(8,128)} async-done(((f32[96,1536]{1,0:T(8,128)}), f32[768,1536]{1,0:T(8,128)}) %all-gather.12.cloned.1.call-update) | async-done | bytes 4718608 | tf_op jit(solution)/shard_map/all_gather | solution.py:352
  1734.4 142.8 %all-gather.10.cloned.1.call-done = f32[384,6400]{1,0:T(8,128)} async-done(((f32[48,6400]{1,0:T(8,128)}), f32[384,6400]{1,0:T(8,128)}) %all-gather.10.cloned.1.call-update) | async-done | bytes 9830416 | tf_op jit(solution)/shard_map/all_gather | solution.py:346
  (635 shorter events, 496.2 us)
Async XLA Ops:
  7.2 524.3 %all-gather.8.cloned.1.call-start = ((), (), s32[]{:S(2)}) async-start(), calls=%async_computation.13 | async-start | bytes 11796480 | tf_op jit(solution)/shard_map/all_gather | solution.py:156
  7.2 8.7 collective-permute-start
  32.9 266.3 %copy-start.50 = (bf16[384,48]{0,1:T(8,128)(2,1)S(1)}, bf16[384,48]{0,1:T(8,128)(2,1)}, u32[]{:S(2)}) copy-start(bf16[384,48]{0,1:T(8,128)(2,1)} %param.18) | copy-start | bytes 110596
  32.9 271.8 %copy-start.11 = (bf16[1,128,1536]{2,1,0:T(8,128)(2,1)S(1)}, bf16[1,128,1536]{2,1,0:T(8,128)(2,1)}, u32[]{:S(2)}) copy-start(bf16[1,128,1536]{2,1,0:T(8,128)(2,1)} %param.16) | copy-start | bytes 1179652
  32.9 279.5 %collective-permute-start.1 = (bf16[2,384,6400]{2,1,0:T(8,128)(2,1)}, bf16[2,384,6400]{2,1,0:T(8,128)(2,1)}, u32[]{:S(2)}, u32[]{:S(2)}) collective-permute-start(bf16[2,384,6400]{2,1,0:T(8,128)(2,1)} %pad_maximum_fusion.1), channel_id=1, source_target_pairs={{0,2},{1,3},{2,0},{3,1},{4,6},{5,7},{6,4},{7,5},{8,10},{9,11},{10,... | collective-permute-start | bytes 29491208 | tf_op jit(solution)/shard_map/ppermute | solution.py:22
  306.4 31.8 %all-to-all-start = ((bf16[128,8,6]{0,2,1:T(8,128)(2,1)}), bf16[128,8,6]{0,2,1:T(8,128)(2,1)S(1)}, u32[]{:S(2)}, u32[]{:S(2)}) async-start(bf16[128,8,6]{0,2,1:T(8,128)(2,1)} %all_to_all.106), calls=%async_computation | async-start | bytes 32768 | tf_op jit(solution)/shard_map/all_to_all | solution.py:194
  339.0 20.4 %all-to-all-start.2 = ((bf16[128,8,256]{2,0,1:T(8,128)(2,1)}), bf16[128,8,256]{2,0,1:T(8,128)(2,1)S(1)}, u32[]{:S(2)}, u32[]{:S(2)}) async-start(bf16[128,8,256]{2,0,1:T(8,128)(2,1)} %tile.28), calls=%async_computation.2 | async-start | bytes 1048576 | tf_op jit(solution)/shard_map/all_to_all | solution.py:195
  359.5 24.0 %all-to-all-start.1 = ((bf16[128,8,384]{2,0,1:T(8,128)(2,1)}), bf16[128,8,384]{2,0,1:T(8,128)(2,1)S(1)}, u32[]{:S(2)}, u32[]{:S(2)}) async-start(bf16[128,8,384]{2,0,1:T(8,128)(2,1)} %bitcast.450), calls=%async_computation.1 | async-start | bytes 1572864 | tf_op jit(solution)/shard_map/all_to_all | solution.py:187
  383.5 113.4 %all-to-all-start.3 = ((bf16[128,8,384]{0,2,1:T(8,128)(2,1)}), bf16[128,8,384]{0,2,1:T(8,128)(2,1)}, u32[]{:S(2)}, u32[]{:S(2)}) async-start(bf16[128,8,384]{0,2,1:T(8,128)(2,1)} %bitcast.20), calls=%async_computation.3 | async-start | bytes 1572864 | tf_op jit(solution)/shard_map/all_to_all | solution.py:186
  505.6 25.3 %all-to-all-start.4 = ((bf16[8,128,384]{2,1,0:T(8,128)(2,1)}), bf16[8,128,384]{2,1,0:T(8,128)(2,1)S(1)}, u32[]{:S(2)}, u32[]{:S(2)}) async-start(bf16[8,128,384]{2,1,0:T(8,128)(2,1)} %bitcast.613), calls=%async_computation.4 | async-start | bytes 1572864 | tf_op jit(solution)/shard_map/all_to_all | solution.py:227
  543.8 24.0 %all-to-all-start.5 = ((bf16[128,8,384]{0,2,1:T(8,128)(2,1)}), bf16[128,8,384]{0,2,1:T(8,128)(2,1)}, u32[]{:S(2)}, u32[]{:S(2)}) async-start(bf16[128,8,384]{0,2,1:T(8,128)(2,1)} %bitcast.617), calls=%async_computation.5 | async-start | bytes 1572864 | tf_op jit(solution)/shard_map/all_to_all | solution.py:240
  548.0 298.5 %reduce-scatter.8.cloned.1.call-start = ((), (), s32[]{:S(2)}) async-start(), calls=%async_computation.14 | async-start | bytes 589824 | tf_op jit(solution)/shard_map/reduce_scatter | solution.py:265
  774.2 279.2 %reduce-scatter.12.cloned.1.call-start = ((), (), s32[]{:S(2)}) async-start(), calls=%async_computation.17 | async-start | bytes 19464192 | tf_op jit(solution)/shard_map/reduce_scatter | solution.py:338
  796.3 22.8 %all-to-all-start.6 = ((bf16[8,128,384]{2,1,0:T(8,128)(2,1)}), bf16[8,128,384]{2,1,0:T(8,128)(2,1)S(1)}, u32[]{:S(2)}, u32[]{:S(2)}) async-start(bf16[8,128,384]{2,1,0:T(8,128)(2,1)} %bitcast.31), calls=%async_computation.6 | async-start | bytes 1572864 | tf_op jit(solution)/shard_map/all_to_all | solution.py:251
  819.1 26.1 %all-to-all-start.7 = ((bf16[8,128,384]{2,1,0:T(8,128)(2,1)}), bf16[8,128,384]{2,1,0:T(8,128)(2,1)S(1)}, u32[]{:S(2)}, u32[]{:S(2)}) async-start(bf16[8,128,384]{2,1,0:T(8,128)(2,1)} %bitcast.35), calls=%async_computation.7 | async-start | bytes 1572864 | tf_op jit(solution)/shard_map/all_to_all | solution.py:254
  822.8 594.8 %reduce-scatter.10.cloned.1.call-start = ((), (), s32[]{:S(2)}) async-start(), calls=%async_computation.15 | async-start | bytes 40550400 | tf_op jit(solution)/shard_map/reduce_scatter | solution.py:295
  912.8 637.1 %all-reduce.33.cloned.1.call-start = ((), (), s32[]{:S(2)}) async-start(), calls=%async_computation.20 | async-start | bytes 192512
  920.7 732.1 %reduce-scatter.14.cloned.1.call-start = ((), (), s32[]{:S(2)}) async-start(), calls=%async_computation.19 | async-start | bytes 811008 | tf_op jit(solution)/shard_map/reduce_scatter | solution.py:301
  921.9 495.6 %copy-start.70 = (u32[32]{0:T(128)S(1)}, u32[32]{0:T(128)}, u32[]{:S(2)}) copy-start(u32[32]{0:T(128)} %constant.207) | copy-start | bytes 388
  921.9 498.2 %copy-start.13 = (bf16[1,128,1536]{2,1,0:T(8,128)(2,1)S(1)}, bf16[1,128,1536]{2,1,0:T(8,128)(2,1)}, u32[]{:S(2)}) copy-start(bf16[1,128,1536]{2,1,0:T(8,128)(2,1)} %param.16) | copy-start | bytes 1179652
  921.9 498.2 %copy-start.32 = (f32[4,1,768]{2,1,0:T(1,128)S(1)}, f32[4,1,768]{2,1,0:T(1,128)}, u32[]{:S(2)}) copy-start(f32[4,1,768]{2,1,0:T(1,128)} %copy-done.31) | copy-start | bytes 36868
  921.9 498.2 %copy-start.57 = (f32[128]{0:T(128)S(1)}, f32[128]{0:T(128)}, u32[]{:S(2)}) copy-start(f32[128]{0:T(128)} %copy-done.56) | copy-start | bytes 1540
  922.0 812.4 %all-gather.12.cloned.1.call-start = ((), (), s32[]{:S(2)}) async-start(), calls=%async_computation.18 | async-start | bytes 5308416 | tf_op jit(solution)/shard_map/all_gather | solution.py:352
  1053.5 823.7 %all-gather.10.cloned.1.call-start = ((), (), s32[]{:S(2)}) async-start(), calls=%async_computation.16 | async-start | bytes 11059200 | tf_op jit(solution)/shard_map/all_gather | solution.py:346
  (75 other events, 1019.1 us)
Sparse Core Ops, SparseCore 0:
  35.9 115.1 all-gather.7
  774.3 68.4 reduce-scatter.7
  849.3 204.1 reduce-scatter.11
  1059.7 357.7 reduce-scatter.9
  1424.9 124.8 all-reduce.32
  1555.4 97.3 reduce-scatter.13
  1655.0 79.3 all-gather.11
  1736.6 140.5 all-gather.9
